TPU v7x, 32 devices: a whole 2x2x4 slice. The times are simulated.
32 devices in a mesh: dp: 8 (over y, x, core), mp: 4 (over z).
Axes of the slice: x: 2, y: 2, z: 4, core: 2. Of those that a mesh axis runs over, the one named last changes fastest.
Arguments:
- tokens: bfloat16 [16384, 1024], P(('dp', 'mp')), may hold values from -6 to 6
- norm_gain: float32 [2, 1024], replicated, may hold values from 0.1 to 1.9
- qkv_weight: bfloat16 [3, 1024, 1024], P(None, 'dp', 'mp')
- out_weight: bfloat16 [1024, 1024], P('mp', 'dp'), may hold values from -0.1875 to 0.1875
- variate_bias: float32 [2, 16], replicated, may hold values from -6 to 6
- ffn_weight: bfloat16 [2, 1024, 2816], P(None, 'dp', 'mp'), may hold values from -0.1875 to 0.1875
- down_weight: bfloat16 [2816, 1024], P('mp', 'dp'), may hold values from -0.109375 to 0.109375
- sample_ids: int32 [16384], P(('dp', 'mp')), may hold values from 0 to 127, as said below
- variate_ids: int32 [16384], P(('dp', 'mp')), may hold values from 0 to 15, as said below
- time_ids: int32 [16384], P(('dp', 'mp')), may hold values from 0 to 31, as said below
Outputs:
- encoded: bfloat16 [16384, 1024], P(('dp', 'mp'))
Inputs may be any that keep to these rules, and one draw needn't show every extreme that they name: `sample_ids`: within each packed sequence of 512 tokens the series numbers start at 0 and never fall; a series with v variates (1 to 16) and p patches (4 to 32) holds v * p consecutive tokens, the last series of a sequence may be cut short; some packed sequence holds 128 series of one variate and four patches each. `variate_ids`: A token's offset within its series divided by that series' patch count p. `time_ids`: A token's offset within its series modulo that series' patch count p.
All inputs are finite; a program needn't handle non-finite values.
Results may differ from a plain program's by a relative error of at most 0.017.
Values may be sent and summed in bfloat16 or wider, within the bound.
A program may use at most 128 MiB of HBM per device.

v0:
```python
import jax
import jax.numpy as jnp
from jax import lax
from jax.sharding import PartitionSpec as P

HEAD_DIM = 64
L = 512


def rms_norm(values, gain):
    wide = values.astype(jnp.float32)
    square = jnp.mean(wide * wide, axis=-1, keepdims=True)
    return (wide * lax.rsqrt(square + 1e-05) * gain[None, :]).astype(jnp.bfloat16)


def rotate(values, times):
    half = values.shape[-1] // 2
    freq = 10000.0 ** (-jnp.arange(half, dtype=jnp.float32) / half)
    angle = times.astype(jnp.float32)[:, None] * freq[None, :]
    cosine = jnp.cos(angle)[:, None, :]
    sine = jnp.sin(angle)[:, None, :]
    first = values[..., :half]
    second = values[..., half:]
    return jnp.concatenate(
        [first * cosine - second * sine, first * sine + second * cosine], axis=-1
    )


def rotated(raw, times):
    row_total, local_width = raw.shape
    turned = rotate(raw.reshape(row_total, local_width // HEAD_DIM, HEAD_DIM), times)
    return turned.reshape(row_total, local_width).astype(jnp.bfloat16)


def attend(queries, keys_rot, values, samples, variates, bias):
    row_total, local_width = queries.shape
    heads_here = local_width // HEAD_DIM
    count = row_total // L

    def one_sequence(args):
        qs, ks, vs, sample_row, variate_row = args
        scores = jnp.einsum(
            "qhd,khd->hqk", qs, ks, preferred_element_type=jnp.float32
        ) * HEAD_DIM ** (-0.5)
        same = variate_row[:, None] == variate_row[None, :]
        scores = scores + jnp.where(same[None], bias[0][:, None, None], bias[1][:, None, None])
        scores = jnp.where((sample_row[:, None] == sample_row[None, :])[None], scores, -1e30)
        top = jnp.max(scores, axis=2, keepdims=True)
        expo = jnp.exp(scores - top)
        weights = (expo / jnp.sum(expo, axis=2, keepdims=True)).astype(jnp.bfloat16)
        return jnp.einsum("hqk,khd->qhd", weights, vs, preferred_element_type=jnp.float32).astype(
            jnp.bfloat16
        )

    shape = (count, L, heads_here, HEAD_DIM)
    result = lax.map(
        one_sequence,
        (
            queries.reshape(shape),
            keys_rot.reshape(shape),
            values.reshape(shape),
            samples.reshape(count, L),
            variates.reshape(count, L),
        ),
    )
    return result.reshape(row_total, local_width)


def local(
    tokens,
    norm_gain,
    qkv_weight,
    out_weight,
    variate_bias,
    ffn_weight,
    down_weight,
    sample_ids,
    variate_ids,
    time_ids,
):
    first_normed = rms_norm(tokens, norm_gain[0])
    wide_columns = lax.all_gather(qkv_weight, "mp", axis=2, tiled=True)
    columns = first_normed
    projected = jnp.einsum(
        "rc,jcd->jrd",
        columns,
        lax.all_gather(wide_columns, "dp", axis=1, tiled=True),
        preferred_element_type=jnp.float32,
    )
    queries = rotated(projected[0], time_ids)
    keys_rot = rotated(projected[1], time_ids)
    values = projected[2].astype(jnp.bfloat16)
    back_rows = attend(queries, keys_rot, values, sample_ids, variate_ids, variate_bias)
    out_rows = lax.all_gather(out_weight, "mp", axis=0, tiled=True)
    mixed = jnp.dot(
        back_rows,
        lax.all_gather(out_rows, "dp", axis=1, tiled=True),
        preferred_element_type=jnp.float32,
    )
    residual = (tokens.astype(jnp.float32) + mixed).astype(jnp.bfloat16)
    second_normed = rms_norm(residual, norm_gain[1])
    ffn_columns = lax.all_gather(ffn_weight, "mp", axis=2, tiled=True)
    columns = second_normed
    gate_up = jnp.einsum(
        "rc,jcf->jrf",
        columns,
        lax.all_gather(ffn_columns, "dp", axis=1, tiled=True),
        preferred_element_type=jnp.float32,
    )
    hidden = (jax.nn.silu(gate_up[0]) * gate_up[1]).astype(jnp.bfloat16)
    down_full = lax.all_gather(down_weight, "mp", axis=0, tiled=True)
    feed = jnp.dot(
        hidden,
        lax.all_gather(down_full, "dp", axis=1, tiled=True),
        preferred_element_type=jnp.float32,
    )
    return (residual.astype(jnp.float32) + feed).astype(jnp.bfloat16)


def solution(mesh):
    return jax.shard_map(
        local,
        mesh=mesh,
        in_specs=(
            P(("dp", "mp"), None),
            P(),
            P(None, "dp", "mp"),
            P("mp", "dp"),
            P(),
            P(None, "dp", "mp"),
            P("mp", "dp"),
            P(("dp", "mp")),
            P(("dp", "mp")),
            P(("dp", "mp")),
        ),
        out_specs=P(("dp", "mp"), None),
        check_vma=False,
    )
```

profile of v0, /device:TPU:0, one launch (start us, length us, event | category | flops | bytes accessed | tf_op | source)
XLA Modules:
  0.0 265.7 jit_solution(9024680529559725444)
XLA Ops:
  6.6 2.2 copy.27
  8.9 27.7 %all_gather.24 = bf16[3,128,1024]{2,1,0:T(8,128)(2,1)} all-gather(bf16[3,128,256]{2,1,0:T(8,128)(2,1)} %param.12), channel_id=1, replica_groups=mesh['dp'=8,'mp'=4] {'mp'}, dimensions={2}, use_global_device_ids=true | all-gather | bytes 983040 | tf_op jit(solution)/shard_map/all_gather | solution.py:82
  36.7 19.0 %all_gather.26 = bf16[1024,128]{1,0:T(8,128)(2,1)} all-gather(bf16[256,128]{1,0:T(8,128)(2,1)} %param.13), channel_id=1, replica_groups=mesh['dp'=8,'mp'=4] {'mp'}, dimensions={0}, use_global_device_ids=true | all-gather | bytes 327680 | tf_op jit(solution)/shard_map/all_gather | solution.py:94
  55.7 1.1 all-gather.10.cloned.1.call-done
  56.9 4.9 %copy.28 = bf16[2,128,2816]{2,1,0:T(8,128)(2,1)} copy(bf16[2,128,2816]{1,0,2:T(2,128)(2,1)} %all-gather.10.cloned.1.call-done) | data formatting | bytes 2883584 | tf_op jit(solution)/shard_map/all_gather | solution.py:102
  61.8 18.1 %all_gather.30 = bf16[2816,128]{1,0:T(8,128)(2,1)} all-gather(bf16[704,128]{1,0:T(8,128)(2,1)S(1)} %copy-done.3), channel_id=1, replica_groups=mesh['dp'=8,'mp'=4] {'mp'}, dimensions={0}, use_global_device_ids=true | all-gather | bytes 901120 | tf_op jit(solution)/shard_map/all_gather | solution.py:111
  80.0 0.3 fusion.15
  80.3 0.3 multiply_cosine_fusion
  80.6 1.1 broadcast_compare_fusion
  81.7 21.9 %all-gather.6.cloned.1.call-done = bf16[3,1024,1024]{2,1,0:T(8,128)(2,1)} async-done(((bf16[3,128,1024]{2,1,0:T(8,128)(2,1)}), bf16[3,1024,1024]{2,1,0:T(8,128)(2,1)}) %all-gather.6.cloned.1.call-update) | async-done | bytes 6291472 | tf_op jit(solution)/shard_map/all_gather | solution.py:87
  103.6 5.7 %convolution_bitcast_fusion.1 = f32[3,512,1024]{2,1,0:T(8,128)S(1)} fusion(bf16[3,1024,1024]{2,1,0:T(8,128)(2,1)} %all-gather.6.cloned.1.call-done, bf16[512,1024]{1,0:T(8,128)(2,1)S(1)} %copy-done, f32[1024]{0:T(1024)S(1)} %bitcast.48, f32[512]{0:T(512)S(1)} %add_rsqrt_fusion.1), kind=kOutput, calls=%fused_computation.25 | convolution fusion | flops 3223322624 | bytes 13637632 | tf_op jit(solution)/shard_map/rc,jcd->jrd/dot_general | solution.py:84
  109.3 0.2 slice.89
  109.4 2.4 fusion.49
  111.9 2.0 copy.24
  113.8 2.9 %copy.25 = f32[1,512,1024]{1,2,0:T(8,128)} copy(f32[1,512,1024]{2,1,0:T(8,128)} %get-tuple-element.20) | data formatting | bytes 4194304 | tf_op jit(solution)/shard_map/slice | solution.py:91
  116.8 1.3 copy.23
  118.1 3.2 %subtract_convert_fusion.1 = (bf16[512,16,32]{0,2,1:T(8,128)(2,1)S(1)}, bf16[512,16,32]{0,2,1:T(8,128)(2,1)S(1)}, bf16[512,16,32]{0,2,1:T(8,128)(2,1)}, bf16[512,16,32]{0,2,1:T(8,128)(2,1)}) fusion(f32[512,16,64]{0,2,1:T(8,128)S(1)} %bitcast.44, f32[512,32]{0,1:T(8,128)S(1)} %get-tuple-element.40, f32[512,32]{0,1:T(8,128)S(1)} %get-tuple-element.39, ...), kind=kLoop, calls=%fused_computation.45 | loop fusion | flops 4194304 | bytes 6422528 | tf_op jit(solution)/shard_map/convert.2
  121.3 9.0 %fusion.51 = f32[16,512]{1,0:T(8,128)S(1)} fusion(f32[16]{0:T(128)S(1)} %get-tuple-element.42, f32[16]{0:T(128)S(1)} %get-tuple-element.41, pred[512,512]{0,1:T(8,128)(4,1)S(1)} %get-tuple-element.45, pred[512,512]{0,1:T(8,128)(4,1)} %get-tuple-element.46, bf16[512,16,32]{0,2,1:T(8,128)(2,1)} %get-tuple-element.34, ...), kind=kOutput, calls=%fused_computation.69 | convolution fusion | flops 566231552 | bytes 2654336 | tf_op jit(solution)/shard_map/while/body/eval_jaxpr/sub | solution.py:49
  130.3 11.1 %fusion.25 = bf16[16,64,512]{2,1,0:T(8,128)(2,1)} fusion(bf16[512,16,64]{0,2,1:T(8,128)(2,1)S(1)} %bitcast.46, f32[16,512]{1,0:T(8,128)S(1)} %fusion.51, f32[16]{0:T(128)S(1)} %get-tuple-element.42, f32[16]{0:T(128)S(1)} %get-tuple-element.41, pred[512,512]{0,1:T(8,128)(4,1)S(1)} %get-tuple-element.45, pred[512,512]{0,1:T(8,128)(4,1)} %get-tuple-element.46, ...), kind=kOutput, calls=%fused_computation.35 | convolution fusion | flops 1107829248 | bytes 4751488 | tf_op jit(solution)/shard_map/while/body/eval_jaxpr/hqk,khd->qhd/dot_general | solution.py:51
  141.4 3.8 %fusion.19 = (f32[512]{0:T(512)S(1)}, bf16[512,1024]{1,0:T(8,128)(2,1)S(1)}) fusion(bf16[512,1024]{0,1:T(8,128)(2,1)} %bitcast.49, bf16[1024,1024]{1,0:T(8,128)(2,1)} %all-gather.8.cloned.1.call-done, bf16[512,1024]{1,0:T(8,128)(2,1)S(1)} %copy-done.1), kind=kOutput, calls=%fused_computation.30 | convolution fusion | flops 1076887040 | bytes 5244928 | tf_op jit(solution)/shard_map/dot_general | solution.py:95
  145.2 57.8 %all-gather.12.cloned.1.call-done = bf16[2,1024,2816]{2,1,0:T(8,128)(2,1)} async-done(((bf16[2,128,2816]{2,1,0:T(8,128)(2,1)}), bf16[2,1024,2816]{2,1,0:T(8,128)(2,1)}) %all-gather.12.cloned.1.call-update) | async-done | bytes 11534352 | tf_op jit(solution)/shard_map/all_gather | solution.py:107
  202.9 13.3 %convolution_bitcast_fusion = f32[2,512,2816]{2,1,0:T(8,128)} fusion(bf16[2,1024,2816]{2,1,0:T(8,128)(2,1)} %all-gather.12.cloned.1.call-done, bf16[512,1024]{1,0:T(8,128)(2,1)S(1)} %get-tuple-element.44, f32[1024]{0:T(1024)S(1)} %bitcast.47, f32[512]{0:T(512)S(1)} %add_rsqrt_fusion), kind=kOutput, calls=%fused_computation.12 | convolution fusion | flops 5907677184 | bytes 24123392 | tf_op jit(solution)/shard_map/rc,jcf->jrf/dot_general | solution.py:104
  216.2 32.7 %all-gather.14.cloned.1.call-done = bf16[2816,1024]{1,0:T(8,128)(2,1)} async-done(((bf16[2816,128]{1,0:T(8,128)(2,1)}), bf16[2816,1024]{1,0:T(8,128)(2,1)}) %all-gather.14.cloned.1.call-update) | async-done | bytes 5767184 | tf_op jit(solution)/shard_map/all_gather | solution.py:114
  249.0 10.2 %fusion.22 = bf16[512,1024]{1,0:T(8,128)(2,1)} fusion(bf16[512,1024]{1,0:T(8,128)(2,1)S(1)} %get-tuple-element.44, bf16[2816,1024]{1,0:T(8,128)(2,1)} %all-gather.14.cloned.1.call-done, f32[2,512,2816]{2,1,0:T(8,128)} %convolution_bitcast_fusion), kind=kOutput, calls=%fused_computation.33 | convolution fusion | flops 2963013632 | bytes 19398656 | tf_op jit(solution)/shard_map/dot_general | solution.py:112
  (35 shorter events, 0.4 us)
Async XLA Ops:
  6.5 55.3 %copy-start.3 = (bf16[704,128]{1,0:T(8,128)(2,1)S(1)}, bf16[704,128]{1,0:T(8,128)(2,1)}, u32[]{:S(2)}) copy-start(bf16[704,128]{1,0:T(8,128)(2,1)} %param.16) | copy-start | bytes 540676
  6.5 73.4 %copy-start.7 = (s32[512]{0:T(512)S(1)}, s32[512]{0:T(512)}, u32[]{:S(2)}) copy-start(s32[512]{0:T(512)} %param.19) | copy-start | bytes 6148
  6.5 73.4 %copy-start = (bf16[512,1024]{1,0:T(8,128)(2,1)S(1)}, bf16[512,1024]{1,0:T(8,128)(2,1)}, u32[]{:S(2)}) copy-start(bf16[512,1024]{1,0:T(8,128)(2,1)} %param.10) | copy-start | bytes 3145732
  6.5 73.7 %copy-start.8 = (f32[2,16]{1,0:T(2,128)S(1)}, f32[2,16]{1,0:T(2,128)}, u32[]{:S(2)}) copy-start(f32[2,16]{1,0:T(2,128)} %param.14) | copy-start | bytes 388
  6.5 73.7 %copy-start.6 = (f32[2,1024]{1,0:T(2,128)S(1)}, f32[2,1024]{1,0:T(2,128)}, u32[]{:S(2)}) copy-start(f32[2,1024]{1,0:T(2,128)} %param.11) | copy-start | bytes 24580
  6.5 74.1 %copy-start.5 = (s32[512]{0:T(512)S(1)}, s32[512]{0:T(512)}, u32[]{:S(2)}) copy-start(s32[512]{0:T(512)} %param.17) | copy-start | bytes 6148
  6.6 74.1 %copy-start.4 = (s32[512]{0:T(512)S(1)}, s32[512]{0:T(512)}, u32[]{:S(2)}) copy-start(s32[512]{0:T(512)} %param.18) | copy-start | bytes 6148
  6.6 50.3 %all-gather.10.cloned.1.call-start = ((), (), s32[]{:S(2)}) async-start(), calls=%async_computation.2 | async-start | bytes 1802240 | tf_op jit(solution)/shard_map/all_gather | solution.py:102
  8.8 94.8 %all-gather.6.cloned.1.call-start = ((), (), s32[]{:S(2)}) async-start(), calls=%async_computation | async-start | bytes 7077888 | tf_op jit(solution)/shard_map/all_gather | solution.py:87
  36.6 104.8 %all-gather.8.cloned.1.call-start = ((), (), s32[]{:S(2)}) async-start(), calls=%async_computation.1 | async-start | bytes 2359296 | tf_op jit(solution)/shard_map/all_gather | solution.py:97
  55.7 147.3 %all-gather.12.cloned.1.call-start = ((), (), s32[]{:S(2)}) async-start(), calls=%async_computation.3 | async-start | bytes 12976128 | tf_op jit(solution)/shard_map/all_gather | solution.py:107
  61.8 187.2 %all-gather.14.cloned.1.call-start = ((), (), s32[]{:S(2)}) async-start(), calls=%async_computation.4 | async-start | bytes 6488064 | tf_op jit(solution)/shard_map/all_gather | solution.py:114
  121.3 9.0 %copy-start.2 = (bf16[1,512,1024]{1,2,0:T(8,128)(2,1)S(1)}, bf16[1,512,1024]{1,2,0:T(8,128)(2,1)}, u32[]{:S(2)}) copy-start(bf16[1,512,1024]{1,2,0:T(8,128)(2,1)} %copy.23) | copy-start | bytes 3145732
  130.3 11.1 %copy-start.1 = (bf16[512,1024]{1,0:T(8,128)(2,1)S(1)}, bf16[512,1024]{1,0:T(8,128)(2,1)}, u32[]{:S(2)}) copy-start(bf16[512,1024]{1,0:T(8,128)(2,1)} %param.10) | copy-start | bytes 3145732
Sparse Core Ops, SparseCore 0:
  8.9 47.8 all-gather.9
  58.8 44.7 all-gather.5
  105.5 28.0 all-gather.7
  135.4 67.5 all-gather.11
  204.7 44.2 all-gather.13
where the time goes:
time: 266 us
  waiting for transfers between devices  114 us (43%)
  blocking collectives  64.8 us (24%)
  matrix products  53 us (20%)
  local copies, waits for them, and re-layouts  15.9 us (6%)
  between operations  13.3 us (5%)
  other arithmetic  4.88 us (2%)
    all_gather x1, waiting for transfers between devices, local(): lax.all_gather(ffn_columns, 'dp', axis=1, tiled=True)  57.8 us
    all_gather x1, waiting for transfers between devices, local(): lax.all_gather(down_full, 'dp', axis=1, tiled=True)  32.7 us
    all_gather x1, blocking collectives, local(): wide_columns = lax.all_gather(qkv_weight, 'mp', axis=2, tiled=True)  27.7 us
    all_gather x1, waiting for transfers between devices, local(): lax.all_gather(wide_columns, 'dp', axis=1, tiled=True)  21.9 us
    all_gather x1, blocking collectives, local(): out_rows = lax.all_gather(out_weight, 'mp', axis=0, tiled=True)  19 us
    all_gather x1, blocking collectives, local(): down_full = lax.all_gather(down_weight, 'mp', axis=0, tiled=True)  18.1 us
    dot_general x1, matrix products, local(): jnp.einsum('rc,jcf->jrf', columns, lax.all_gather(ffn_columns, 'dp', axis...  13.3 us
    dot_general x1, matrix products, one_sequence(): jnp.einsum('hqk,khd->qhd', weights, vs, preferred_element_type=jnp.float32)  11.1 us
  transfers between devices with their start and end apart: 5, of which 4 were waited for; matrix products, arithmetic and copies ran while one was open for 23% of the time, Pallas kernels for 0%

commit v1 on v0

--- a/solution.py
+++ b/solution.py
@@ -101,12 +101,38 @@
     second_normed = rms_norm(residual, norm_gain[1])
     ffn_columns = lax.all_gather(ffn_weight, "mp", axis=2, tiled=True)
     columns = second_normed
-    gate_up = jnp.einsum(
+    size, mine, rows = (lax.axis_size("dp"), lax.axis_index("dp"), ffn_columns.shape[1])
+    upward = [(i, (i + 1) % size) for i in range(size)]
+    left = [(i, (i - 1) % size) for i in range(size)]
+    middle = size // 2
+    from_left = from_right = ffn_columns
+    total = jnp.einsum(
         "rc,jcf->jrf",
-        columns,
-        lax.all_gather(ffn_columns, "dp", axis=1, tiled=True),
+        lax.dynamic_slice_in_dim(columns, mine * rows, ffn_columns.shape[1], axis=1),
+        ffn_columns,
         preferred_element_type=jnp.float32,
     )
+    for step in range(1, middle + 1):
+        from_left = lax.ppermute(from_left, "dp", upward)
+        if step < size - middle:
+            from_right = lax.ppermute(from_right, "dp", left)
+            total = total + jnp.einsum(
+                "rc,jcf->jrf",
+                lax.dynamic_slice_in_dim(
+                    columns, (mine + step) % size * rows, from_right.shape[1], axis=1
+                ),
+                from_right,
+                preferred_element_type=jnp.float32,
+            )
+        total = total + jnp.einsum(
+            "rc,jcf->jrf",
+            lax.dynamic_slice_in_dim(
+                columns, (mine - step) % size * rows, from_left.shape[1], axis=1
+            ),
+            from_left,
+            preferred_element_type=jnp.float32,
+        )
+    gate_up = total
     hidden = (jax.nn.silu(gate_up[0]) * gate_up[1]).astype(jnp.bfloat16)
     down_full = lax.all_gather(down_weight, "mp", axis=0, tiled=True)
     feed = jnp.dot(

time: 266 us -> 308 us (1.16)
  matrix products: 53 us -> 117 us
  waiting for transfers between devices: 114 us -> 91.2 us
  local copies, waits for them, and re-layouts: 15.9 us -> 9.76 us
  starting transfers between devices: 0.21 us -> 6.28 us
    ppermute x0 -> x7, waiting for transfers between devices: none -> 87.7 us  [the longest x4 83.6 us: local(): from_left = lax.ppermute(from_left, 'dp', upward)]
    dot_general x1 -> x8, matrix products: 13.3 us -> 76.5 us  [the longest x4 50.1 us: local(): jnp.einsum('rc,jcf->jrf', lax.dynamic_slice_in_dim(columns, (mine - step)...]
    all_gather x1 -> x0, waiting for transfers between devices: 57.8 us -> none  [local(): lax.all_gather(ffn_columns, 'dp', axis=1, tiled=True)]
    all_gather x1, waiting for transfers between devices: 32.7 us -> 0.01 us  [local(): lax.all_gather(down_full, 'dp', axis=1, tiled=True)]
    all_gather x1, waiting for transfers between devices: 21.9 us -> 0.01 us  [local(): lax.all_gather(wide_columns, 'dp', axis=1, tiled=True)]
    ppermute x0 -> x7, starting transfers between devices: none -> 6.12 us  [the longest x3 6.1 us: local(): from_right = lax.ppermute(from_right, 'dp', left)]
    all_gather x1 -> x0, local copies, waits for them, and re-layouts: 4.91 us -> none  [local(): ffn_columns = lax.all_gather(ffn_weight, 'mp', axis=2, tiled=True)]
  transfers between devices with their start and end apart: 5 -> 11, of which waited for: 4 -> 5; matrix products, arithmetic and copies ran while one was open for 23% -> 40% of each run, Pallas kernels for 0% -> 0%
where the time goes in v1:
time: 308 us; the launch traced here: 307 us
  matrix products  117 us (38%)
  waiting for transfers between devices  91.2 us (30%)
  blocking collectives  63.4 us (21%)
  between operations  13.5 us (4%)
  local copies, waits for them, and re-layouts  9.76 us (3%)
  other arithmetic  6.35 us (2%)
  starting transfers between devices  6.28 us (2%)
    ppermute x4, waiting for transfers between devices, local(): from_left = lax.ppermute(from_left, 'dp', upward)  83.6 us
    dot_general x4, matrix products, local(): jnp.einsum('rc,jcf->jrf', lax.dynamic_slice_in_dim(columns, (mine - step)...  50.1 us
    all_gather x1, blocking collectives, local(): wide_columns = lax.all_gather(qkv_weight, 'mp', axis=2, tiled=True)  26.3 us
    dot_general x3, matrix products, local(): jnp.einsum('rc,jcf->jrf', lax.dynamic_slice_in_dim(columns, (mine + step)...  20.6 us
    all_gather x1, blocking collectives, local(): out_rows = lax.all_gather(out_weight, 'mp', axis=0, tiled=True)  18.8 us
    all_gather x1, blocking collectives, local(): down_full = lax.all_gather(down_weight, 'mp', axis=0, tiled=True)  18.3 us
    dot_general x1, matrix products, one_sequence(): jnp.einsum('hqk,khd->qhd', weights, vs, preferred_element_type=jnp.float32)  11.1 us
    dot_general x1, matrix products, local(): jnp.dot(hidden, lax.all_gather(down_full, 'dp', axis=1, tiled=True), pref...  10.2 us
  transfers between devices with their start and end apart: 11, of which 5 were waited for; matrix products, arithmetic and copies ran while one was open for 40% of the time, Pallas kernels for 0%

profile of v1, /device:TPU:0, one launch (start us, length us, event | category | flops | bytes accessed | tf_op | source)
XLA Modules:
  0.0 307.1 jit_solution(17564873382233900211)
XLA Ops:
  7.3 26.3 %all_gather.21 = bf16[3,128,1024]{2,1,0:T(8,128)(2,1)} all-gather(bf16[3,128,256]{2,1,0:T(8,128)(2,1)} %param.12), channel_id=1, replica_groups=mesh['dp'=8,'mp'=4] {'mp'}, dimensions={2}, use_global_device_ids=true | all-gather | bytes 983040 | tf_op jit(solution)/shard_map/all_gather | solution.py:82
  33.7 18.8 %all_gather.23 = bf16[1024,128]{1,0:T(8,128)(2,1)} all-gather(bf16[256,128]{1,0:T(8,128)(2,1)} %param.13), channel_id=1, replica_groups=mesh['dp'=8,'mp'=4] {'mp'}, dimensions={0}, use_global_device_ids=true | all-gather | bytes 327680 | tf_op jit(solution)/shard_map/all_gather | solution.py:94
  52.6 2.8 all-gather.9.cloned.1.call-done
  55.4 2.6 collective-permute-start
  58.0 43.2 %collective-permute-done.1 = bf16[2,128,2816]{1,2,0:T(8,128)(2,1)S(1)} collective-permute-done((bf16[2,128,2816]{1,2,0:T(8,128)(2,1)}, bf16[2,128,2816]{1,2,0:T(8,128)(2,1)S(1)}, u32[]{:S(2)}, u32[]{:S(2)}) %collective-permute-start.1) | collective-permute-done | bytes 1441824 | tf_op jit(solution)/shard_map/ppermute | solution.py:116
  102.3 4.0 %collective-permute-done = bf16[2,128,2816]{1,2,0:T(8,128)(2,1)S(1)} collective-permute-done((bf16[2,128,2816]{1,2,0:T(8,128)(2,1)}, bf16[2,128,2816]{1,2,0:T(8,128)(2,1)S(1)}, u32[]{:S(2)}, u32[]{:S(2)}) %collective-permute-start) | collective-permute-done | bytes 1441824 | tf_op jit(solution)/shard_map/ppermute | solution.py:118
  106.4 2.8 collective-permute-start.2
  109.1 38.9 %collective-permute-done.3 = bf16[2,128,2816]{1,2,0:T(8,128)(2,1)S(1)} collective-permute-done((bf16[2,128,2816]{1,2,0:T(8,128)(2,1)S(1)}, bf16[2,128,2816]{1,2,0:T(8,128)(2,1)S(1)}, u32[]{:S(2)}, u32[]{:S(2)}) %collective-permute-start.3) | collective-permute-done | bytes 1441824 | tf_op jit(solution)/shard_map/ppermute | solution.py:116
  148.1 18.3 %all_gather.26 = bf16[2816,128]{1,0:T(8,128)(2,1)} all-gather(bf16[704,128]{1,0:T(8,128)(2,1)} %param.16), channel_id=1, replica_groups=mesh['dp'=8,'mp'=4] {'mp'}, dimensions={0}, use_global_device_ids=true | all-gather | bytes 901120 | tf_op jit(solution)/shard_map/all_gather | solution.py:137
  171.8 6.3 %convolution_bitcast_fusion = f32[3,512,1024]{2,1,0:T(8,128)S(1)} fusion(bf16[3,1024,1024]{2,1,0:T(8,128)(2,1)} %all-gather.5.cloned.1.call-done, bf16[512,1024]{1,0:T(8,128)(2,1)} %param.10, f32[1024]{0:T(1024)S(1)} %bitcast.76, f32[512]{0:T(512)S(1)} %add_rsqrt_fusion.1), kind=kOutput, calls=%fused_computation.25 | convolution fusion | flops 3223322624 | bytes 13637632 | tf_op jit(solution)/shard_map/rc,jcd->jrd/dot_general | solution.py:84
  182.4 2.9 copy.26
  186.7 3.2 %subtract_convert_fusion.1 = (bf16[512,16,32]{0,2,1:T(8,128)(2,1)S(1)}, bf16[512,16,32]{0,2,1:T(8,128)(2,1)S(1)}, bf16[512,16,32]{0,2,1:T(8,128)(2,1)}, bf16[512,16,32]{0,2,1:T(8,128)(2,1)}) fusion(f32[512,16,64]{0,2,1:T(8,128)S(1)} %bitcast.72, f32[512,32]{0,1:T(8,128)S(1)} %get-tuple-element.40, f32[512,32]{0,1:T(8,128)S(1)} %get-tuple-element.39, ...), kind=kLoop, calls=%fused_computation.42 | loop fusion | flops 4194304 | bytes 6422528 | tf_op jit(solution)/shard_map/convert.2
  189.8 9.0 %fusion.78 = f32[16,512]{1,0:T(8,128)S(1)} fusion(f32[16]{0:T(128)S(1)} %get-tuple-element.42, f32[16]{0:T(128)S(1)} %get-tuple-element.41, pred[512,512]{0,1:T(8,128)(4,1)S(1)} %get-tuple-element.45, pred[512,512]{0,1:T(8,128)(4,1)} %get-tuple-element.46, bf16[512,16,32]{0,2,1:T(8,128)(2,1)} %get-tuple-element.34, ...), kind=kOutput, calls=%fused_computation.97 | convolution fusion | flops 566231552 | bytes 2654336 | tf_op jit(solution)/shard_map/while/body/eval_jaxpr/sub | solution.py:49
  198.9 11.1 %fusion.25 = bf16[16,64,512]{2,1,0:T(8,128)(2,1)} fusion(bf16[512,16,64]{0,2,1:T(8,128)(2,1)S(1)} %bitcast.74, f32[16,512]{1,0:T(8,128)S(1)} %fusion.78, f32[16]{0:T(128)S(1)} %get-tuple-element.42, f32[16]{0:T(128)S(1)} %get-tuple-element.41, pred[512,512]{0,1:T(8,128)(4,1)S(1)} %get-tuple-element.45, pred[512,512]{0,1:T(8,128)(4,1)} %get-tuple-element.46, ...), kind=kOutput, calls=%fused_computation.35 | convolution fusion | flops 1107829248 | bytes 4751488 | tf_op jit(solution)/shard_map/while/body/eval_jaxpr/hqk,khd->qhd/dot_general | solution.py:51
  210.0 3.5 %fusion.19 = (f32[512]{0:T(512)S(1)}, bf16[512,1024]{1,0:T(8,128)(2,1)S(1)}) fusion(bf16[512,1024]{0,1:T(8,128)(2,1)} %bitcast.77, bf16[1024,1024]{1,0:T(8,128)(2,1)} %all-gather.7.cloned.1.call-done, bf16[512,1024]{1,0:T(8,128)(2,1)S(1)} %copy-done.7), kind=kOutput, calls=%fused_computation.30 | convolution fusion | flops 1076887040 | bytes 5244928 | tf_op jit(solution)/shard_map/dot_general | solution.py:95
  213.8 6.0 %fusion.36 = f32[512,2,2816]{2,0,1:T(8,128)} fusion(bf16[2,128,2816]{1,2,0:T(8,128)(2,1)S(1)} %copy-done.6, bf16[512,1024]{1,0:T(8,128)(2,1)S(1)} %fusion.21, s32[]{:T(128)S(6)} %select_n.75), kind=kOutput, calls=%fused_computation.53 | convolution fusion | flops 738197504 | bytes 13107204 | tf_op jit(solution)/shard_map/rc,jcf->jrf/dot_general | solution.py:127
  219.8 7.6 %fusion.38 = f32[512,2,2816]{2,0,1:T(8,128)} fusion(bf16[2,128,2816]{1,2,0:T(8,128)(2,1)} %collective-permute-done.2, bf16[512,1024]{1,0:T(8,128)(2,1)S(1)} %fusion.21, s32[]{:T(128)S(6)} %select_n.73), kind=kOutput, calls=%fused_computation.55 | convolution fusion | flops 738197504 | bytes 13107204 | tf_op jit(solution)/shard_map/rc,jcf->jrf/dot_general | solution.py:119
  227.4 5.9 %fusion.40 = f32[512,2,2816]{2,0,1:T(8,128)} fusion(bf16[2,128,2816]{1,2,0:T(8,128)(2,1)S(1)} %copy-done.2, bf16[512,1024]{1,0:T(8,128)(2,1)S(1)} %fusion.21, s32[]{:T(128)S(6)} %select_n.71), kind=kOutput, calls=%fused_computation.57 | convolution fusion | flops 738197504 | bytes 13107204 | tf_op jit(solution)/shard_map/rc,jcf->jrf/dot_general | solution.py:127
  233.3 5.8 %fusion.42 = f32[512,2,2816]{2,0,1:T(8,128)} fusion(bf16[2,128,2816]{1,2,0:T(8,128)(2,1)S(1)} %copy-done.4, bf16[512,1024]{1,0:T(8,128)(2,1)S(1)} %fusion.21, s32[]{:T(128)S(6)} %select_n.69), kind=kOutput, calls=%fused_computation.59 | convolution fusion | flops 738197504 | bytes 13107204 | tf_op jit(solution)/shard_map/rc,jcf->jrf/dot_general | solution.py:119
  239.1 7.5 %fusion.32 = f32[512,2,2816]{2,0,1:T(8,128)} fusion(bf16[2,128,2816]{1,2,0:T(8,128)(2,1)} %collective-permute-done.5, bf16[512,1024]{1,0:T(8,128)(2,1)S(1)} %fusion.21, s32[]{:T(128)S(6)} %select_n.79), kind=kOutput, calls=%fused_computation.49 | convolution fusion | flops 738197504 | bytes 13107204 | tf_op jit(solution)/shard_map/rc,jcf->jrf/dot_general | solution.py:127
  246.6 5.8 %fusion.44 = f32[512,2,2816]{2,0,1:T(8,128)} fusion(bf16[2,128,2816]{1,2,0:T(8,128)(2,1)S(1)} %copy-done, bf16[512,1024]{1,0:T(8,128)(2,1)S(1)} %fusion.21, s32[]{:T(128)S(6)} %select_n.67), kind=kOutput, calls=%fused_computation.61 | convolution fusion | flops 738197504 | bytes 13107204 | tf_op jit(solution)/shard_map/rc,jcf->jrf/dot_general | solution.py:109
  252.5 7.2 %fusion.34 = f32[512,2,2816]{2,0,1:T(8,128)} fusion(bf16[2,128,2816]{1,2,0:T(8,128)(2,1)} %collective-permute-done.4, bf16[512,1024]{1,0:T(8,128)(2,1)S(1)} %fusion.21, s32[]{:T(128)S(6)} %select_n.77), kind=kOutput, calls=%fused_computation.51 | convolution fusion | flops 738197504 | bytes 13107204 | tf_op jit(solution)/shard_map/rc,jcf->jrf/dot_general | solution.py:119
  259.7 30.7 %add_bitcast_fusion = f32[2,512,2816]{2,1,0:T(8,128)} fusion(f32[512,2,2816]{2,0,1:T(8,128)} %fusion.32, f32[512,2,2816]{2,0,1:T(8,128)} %fusion.34, f32[512,2,2816]{2,0,1:T(8,128)} %fusion.36, f32[512,2,2816]{2,0,1:T(8,128)} %fusion.38, f32[512,2,2816]{2,0,1:T(8,128)} %fusion.40, f32[512,2,2816]{2,0,1:T(8,128)} %fusion.44, f32[512,2,2816]{2,0,1:T(8,128)} %fusion.42, ...), kind=kOutput, calls=%fused_computation.5 | convolution fusion | flops 758382592 | bytes 93847552 | tf_op jit(solution)/shard_map/rc,jcf->jrf/dot_general | solution.py:127
  290.3 10.2 %fusion.22 = bf16[512,1024]{1,0:T(8,128)(2,1)} fusion(bf16[512,1024]{1,0:T(8,128)(2,1)S(1)} %get-tuple-element.44, bf16[2816,1024]{1,0:T(8,128)(2,1)} %all-gather.11.cloned.1.call-done, f32[2,512,2816]{2,1,0:T(8,128)} %add_bitcast_fusion), kind=kOutput, calls=%fused_computation.33 | convolution fusion | flops 2963013632 | bytes 19398656 | tf_op jit(solution)/shard_map/dot_general | solution.py:138
  (62 shorter events, 13.2 us)
Async XLA Ops:
  6.5 160.0 %copy-start.12 = (s32[512]{0:T(512)S(1)}, s32[512]{0:T(512)}, u32[]{:S(2)}) copy-start(s32[512]{0:T(512)} %param.19) | copy-start | bytes 6148
  6.5 161.6 %copy-start.13 = (f32[2,16]{1,0:T(2,128)S(1)}, f32[2,16]{1,0:T(2,128)}, u32[]{:S(2)}) copy-start(f32[2,16]{1,0:T(2,128)} %param.14) | copy-start | bytes 388
  6.5 161.6 %copy-start.11 = (f32[2,1024]{1,0:T(2,128)S(1)}, f32[2,1024]{1,0:T(2,128)}, u32[]{:S(2)}) copy-start(f32[2,1024]{1,0:T(2,128)} %param.11) | copy-start | bytes 24580
  6.5 161.9 %copy-start.10 = (s32[512]{0:T(512)S(1)}, s32[512]{0:T(512)}, u32[]{:S(2)}) copy-start(s32[512]{0:T(512)} %param.17) | copy-start | bytes 6148
  6.5 161.9 %copy-start.9 = (s32[512]{0:T(512)S(1)}, s32[512]{0:T(512)}, u32[]{:S(2)}) copy-start(s32[512]{0:T(512)} %param.18) | copy-start | bytes 6148
  6.5 48.8 %all-gather.9.cloned.1.call-start = ((), (), s32[]{:S(2)}) async-start(), calls=%async_computation.2 | async-start | bytes 1802240 | tf_op jit(solution)/shard_map/all_gather | solution.py:102
  7.3 164.5 %all-gather.5.cloned.1.call-start = ((), (), s32[]{:S(2)}) async-start(), calls=%async_computation | async-start | bytes 7077888 | tf_op jit(solution)/shard_map/all_gather | solution.py:87
  33.6 176.3 %all-gather.7.cloned.1.call-start = ((), (), s32[]{:S(2)}) async-start(), calls=%async_computation.1 | async-start | bytes 2359296 | tf_op jit(solution)/shard_map/all_gather | solution.py:97
  52.6 237.8 %all-gather.11.cloned.1.call-start = ((), (), s32[]{:S(2)}) async-start(), calls=%async_computation.3 | async-start | bytes 6488064 | tf_op jit(solution)/shard_map/all_gather | solution.py:140
  55.4 45.8 %collective-permute-start.1 = (bf16[2,128,2816]{1,2,0:T(8,128)(2,1)}, bf16[2,128,2816]{1,2,0:T(8,128)(2,1)S(1)}, u32[]{:S(2)}, u32[]{:S(2)}) collective-permute-start(bf16[2,128,2816]{1,2,0:T(8,128)(2,1)} %all-gather.9.cloned.1.call-done), channel_id=1, source_target_pairs={{0,4},{4,8},{8,12},{12,16},{16,20},{20,24},{24,28},{28,0},{1,5},{5... | collective-permute-start | bytes 4325384 | tf_op jit(solution)/shard_map/ppermute | solution.py:116
  55.4 51.0 %collective-permute-start = (bf16[2,128,2816]{1,2,0:T(8,128)(2,1)}, bf16[2,128,2816]{1,2,0:T(8,128)(2,1)S(1)}, u32[]{:S(2)}, u32[]{:S(2)}) collective-permute-start(bf16[2,128,2816]{1,2,0:T(8,128)(2,1)} %all-gather.9.cloned.1.call-done), channel_id=1, source_target_pairs={{0,28},{4,0},{8,4},{12,8},{16,12},{20,16},{24,20},{28,24},{1,29},{... | collective-permute-start | bytes 4325384 | tf_op jit(solution)/shard_map/ppermute | solution.py:118
  102.3 45.7 %collective-permute-start.3 = (bf16[2,128,2816]{1,2,0:T(8,128)(2,1)S(1)}, bf16[2,128,2816]{1,2,0:T(8,128)(2,1)S(1)}, u32[]{:S(2)}, u32[]{:S(2)}) collective-permute-start(bf16[2,128,2816]{1,2,0:T(8,128)(2,1)S(1)} %collective-permute-done.1), channel_id=1, source_target_pairs={{0,4},{4,8},{8,12},{12,16},{16,20},{20,24},{24,28},{28,0},{1,5},{5... | collective-permute-start | bytes 4325384 | tf_op jit(solution)/shard_map/ppermute | solution.py:116
  106.4 71.7 %copy-start.3 = (bf16[2,128,2816]{1,2,0:T(8,128)(2,1)}, bf16[2,128,2816]{1,2,0:T(8,128)(2,1)S(1)}, u32[]{:S(2)}) copy-start(bf16[2,128,2816]{1,2,0:T(8,128)(2,1)S(1)} %collective-permute-done) | copy-start | bytes 4325380
  106.4 63.1 %collective-permute-start.2 = (bf16[2,128,2816]{1,2,0:T(8,128)(2,1)S(1)}, bf16[2,128,2816]{1,2,0:T(8,128)(2,1)}, u32[]{:S(2)}, u32[]{:S(2)}) collective-permute-start(bf16[2,128,2816]{1,2,0:T(8,128)(2,1)S(1)} %collective-permute-done), channel_id=1, source_target_pairs={{0,28},{4,0},{8,4},{12,8},{16,12},{20,16},{24,20},{28,24},{1,29},{... | collective-permute-start | bytes 4325384 | tf_op jit(solution)/shard_map/ppermute | solution.py:118
  148.1 23.7 %copy-start.5 = (bf16[2,128,2816]{1,2,0:T(8,128)(2,1)}, bf16[2,128,2816]{1,2,0:T(8,128)(2,1)S(1)}, u32[]{:S(2)}) copy-start(bf16[2,128,2816]{1,2,0:T(8,128)(2,1)S(1)} %collective-permute-done.3) | copy-start | bytes 4325380
  148.1 23.7 %collective-permute-start.5 = (bf16[2,128,2816]{1,2,0:T(8,128)(2,1)S(1)}, bf16[2,128,2816]{1,2,0:T(8,128)(2,1)}, u32[]{:S(2)}, u32[]{:S(2)}) collective-permute-start(bf16[2,128,2816]{1,2,0:T(8,128)(2,1)S(1)} %collective-permute-done.3), channel_id=1, source_target_pairs={{0,4},{4,8},{8,12},{12,16},{16,20},{20,24},{24,28},{28,0},{1,5},{5... | collective-permute-start | bytes 4325384 | tf_op jit(solution)/shard_map/ppermute | solution.py:116
  169.5 83.0 %collective-permute-start.4 = (bf16[2,128,2816]{1,2,0:T(8,128)(2,1)}, bf16[2,128,2816]{1,2,0:T(8,128)(2,1)}, u32[]{:S(2)}, u32[]{:S(2)}) collective-permute-start(bf16[2,128,2816]{1,2,0:T(8,128)(2,1)} %collective-permute-done.2), channel_id=1, source_target_pairs={{0,28},{4,0},{8,4},{12,8},{16,12},{20,16},{24,20},{28,24},{1,29},{... | collective-permute-start | bytes 4325384 | tf_op jit(solution)/shard_map/ppermute | solution.py:118
  171.7 87.9 %collective-permute-start.6 = (bf16[2,128,2816]{1,2,0:T(8,128)(2,1)}, bf16[2,128,2816]{1,2,0:T(8,128)(2,1)}, u32[]{:S(2)}, u32[]{:S(2)}) collective-permute-start(bf16[2,128,2816]{1,2,0:T(8,128)(2,1)} %collective-permute-done.5), channel_id=1, source_target_pairs={{0,4},{4,8},{8,12},{12,16},{16,20},{20,24},{24,28},{28,0},{1,5},{5... | collective-permute-start | bytes 4325384 | tf_op jit(solution)/shard_map/ppermute | solution.py:116
  189.8 9.0 %copy-start.8 = (bf16[1,512,1024]{1,2,0:T(8,128)(2,1)S(1)}, bf16[1,512,1024]{1,2,0:T(8,128)(2,1)}, u32[]{:S(2)}) copy-start(bf16[1,512,1024]{1,2,0:T(8,128)(2,1)} %copy.24) | copy-start | bytes 3145732
  198.8 11.1 %copy-start.7 = (bf16[512,1024]{1,0:T(8,128)(2,1)S(1)}, bf16[512,1024]{1,0:T(8,128)(2,1)}, u32[]{:S(2)}) copy-start(bf16[512,1024]{1,0:T(8,128)(2,1)} %param.10) | copy-start | bytes 3145732
  210.0 3.9 %copy-start.6 = (bf16[2,128,2816]{1,2,0:T(8,128)(2,1)S(1)}, bf16[2,128,2816]{1,2,0:T(8,128)(2,1)}, u32[]{:S(2)}) copy-start(bf16[2,128,2816]{1,2,0:T(8,128)(2,1)} %copy-done.5) | copy-start | bytes 4325380
  219.8 7.6 %copy-start.2 = (bf16[2,128,2816]{1,2,0:T(8,128)(2,1)S(1)}, bf16[2,128,2816]{1,2,0:T(8,128)(2,1)}, u32[]{:S(2)}) copy-start(bf16[2,128,2816]{1,2,0:T(8,128)(2,1)} %copy-done.1) | copy-start | bytes 4325380
  227.4 5.9 %copy-start.4 = (bf16[2,128,2816]{1,2,0:T(8,128)(2,1)S(1)}, bf16[2,128,2816]{1,2,0:T(8,128)(2,1)}, u32[]{:S(2)}) copy-start(bf16[2,128,2816]{1,2,0:T(8,128)(2,1)} %copy-done.3) | copy-start | bytes 4325380
  239.1 7.5 %copy-start = (bf16[2,128,2816]{1,2,0:T(8,128)(2,1)S(1)}, bf16[2,128,2816]{1,2,0:T(8,128)(2,1)}, u32[]{:S(2)}) copy-start(bf16[2,128,2816]{1,2,0:T(8,128)(2,1)} %all-gather.9.cloned.1.call-done) | copy-start | bytes 4325380
  (1 other events, 1.1 us)
Sparse Core Ops, SparseCore 0:
  8.9 46.3 all-gather.8
  57.3 66.0 all-gather.4
  125.3 33.5 all-gather.6
  166.5 60.6 all-gather.10
